TPU v7x, 32 devices: a whole 2x2x4 slice. The times are simulated.
32 devices in a mesh: dp: 8 (over z, y), head: 4 (over x, core).
Axes of the slice: x: 2, y: 2, z: 4, core: 2. Of those that a mesh axis runs over, the one named last changes fastest.
Arguments:
- inputs: bfloat16 [8, 1024, 768], P('dp', 'head'), may hold values from -6 to 6
- norm_gains: bfloat16 [2, 768], replicated, may hold values from 0.5 to 1.5
- norm_shifts: bfloat16 [2, 768], replicated, may hold values from -1.75 to 1.75
- w_qkv: bfloat16 [768, 2304], replicated, may hold values from -0.21875 to 0.21875
- qv_bias: bfloat16 [2, 768], replicated, may hold values from -1.75 to 1.75
- w_out: bfloat16 [768, 768], replicated, may hold values from -1.75 to 1.75
- out_biases: bfloat16 [2, 768], replicated, may hold values from -1.75 to 1.75
- w_up: bfloat16 [768, 3072], replicated, may hold values from -0.21875 to 0.21875
- up_bias: bfloat16 [3072], replicated, may hold values from -1.75 to 1.75
- w_down: bfloat16 [3072, 768], replicated, may hold values from -0.21875 to 0.21875
- lengths: int32 [8, 4], P('dp'), may hold values from 0 to 1024, as said below
- d_out: bfloat16 [8, 1024, 768], P('dp', 'head'), may hold values from -8 to 8
Outputs:
- block_out: bfloat16 [8, 1024, 768], P('dp', 'head')
- grad_inputs: float32 [8, 1024, 768], P('dp', 'head')
- grad_norm_gains: float32 [2, 768], P(None, 'dp')
- grad_norm_shifts: float32 [2, 768], P(None, 'dp')
- grad_qkv: float32 [768, 2304], P(None, 'dp')
- grad_qv_bias: float32 [2, 768], P(None, 'dp')
- grad_out: float32 [768, 768], P(None, 'dp')
- grad_out_biases: float32 [2, 768], P(None, 'dp')
- grad_up: float32 [768, 3072], P(None, 'dp')
- grad_up_bias: float32 [3072], P('dp')
- grad_down: float32 [3072, 768], P(None, 'dp')
Inputs may be any that keep to these rules, and one draw needn't show every extreme that they name: Each slot holds either one image of 1024 patches (lengths 1024, then zeros) or 1 to 4 images of 256 patches in its first entries, then zeros. The first slot holds one image of 1024 patches.
All inputs are finite; a program needn't handle non-finite values.
Results may differ from a plain program's by a relative error of at most 0.014.
Values may be sent and summed in bfloat16 or wider, within the bound.
A program may use at most 256 MiB of HBM per device.

v0:
```python
import jax
import jax.numpy as jnp
from jax import lax
from jax.sharding import PartitionSpec as P

D = 768
HEADS = 12
HDIM = 64
SLOT = 1024
ITEMS = 4
EPSILON = 1e-06


def norm_parts(values, norm_gain, norm_shift):
    average = jnp.mean(values, axis=-1, keepdims=True)
    centered = values - average
    variance = jnp.mean(centered * centered, axis=-1, keepdims=True)
    inverse = lax.rsqrt(variance + EPSILON)
    normal_unit = centered * inverse
    return (normal_unit, inverse, normal_unit * norm_gain + norm_shift)


def norm_back(grad_normed, normal_unit, inverse, norm_gain):
    grad_unit = grad_normed * norm_gain
    first_mean = jnp.mean(grad_unit, axis=-1, keepdims=True)
    second_mean = jnp.mean(grad_unit * normal_unit, axis=-1, keepdims=True)
    return inverse * (grad_unit - first_mean - normal_unit * second_mean)


def exact_gelu(values):
    return jax.nn.gelu(values, approximate=False)


def slot_allowed(lengths_row):
    item_ends = jnp.cumsum(lengths_row)
    positions = jnp.arange(SLOT, dtype=jnp.int32)
    segment = jnp.sum((positions[:, None] >= item_ends[None, :]).astype(jnp.int32), axis=1)
    is_real = positions < item_ends[ITEMS - 1]
    same_item = (segment[:, None] == segment[None, :]) & is_real[None, :]
    return (same_item | (positions[:, None] == positions[None, :]))[None]


def block_scores(query_part, key_part, allowed):
    scores = jnp.einsum("hbqe,hbke->hbqk", query_part, key_part, preferred_element_type=jnp.float32)
    scores = scores * query_part.shape[-1] ** (-0.5)
    return jnp.where(allowed[None], scores, -jnp.inf)


def block_forward(query_part, key_part, value_part, allowed):
    masked = block_scores(query_part, key_part, allowed)
    row_max = jnp.max(masked, axis=-1, keepdims=True)
    weights = jnp.exp(masked - row_max)
    row_sum = jnp.sum(weights, axis=-1, keepdims=True)
    low_weights = (weights / row_sum).astype(jnp.bfloat16)
    mixed_out = jnp.einsum(
        "hbqk,hbke->hbqe", low_weights, value_part, preferred_element_type=jnp.float32
    )
    return (mixed_out.astype(jnp.bfloat16), (row_max + jnp.log(row_sum))[..., 0])


def block_backward(query_part, key_part, value_part, allowed, grad_mixed, log_totals):
    masked = block_scores(query_part, key_part, allowed)
    attn_weights = jnp.exp(masked - log_totals[..., None])
    grad_weights = jnp.einsum(
        "hbqe,hbke->hbqk", grad_mixed, value_part, preferred_element_type=jnp.float32
    )
    row_inner = jnp.sum(attn_weights * grad_weights, axis=-1, keepdims=True)
    grad_scores = (attn_weights * (grad_weights - row_inner)).astype(jnp.bfloat16)
    score_scale = query_part.shape[-1] ** (-0.5)
    grad_query = (
        jnp.einsum("hbqk,hbke->hbqe", grad_scores, key_part, preferred_element_type=jnp.float32)
        * score_scale
    )
    grad_key = (
        jnp.einsum("hbqk,hbqe->hbke", grad_scores, query_part, preferred_element_type=jnp.float32)
        * score_scale
    )
    grad_value = jnp.einsum(
        "hbqk,hbqe->hbke",
        attn_weights.astype(jnp.bfloat16),
        grad_mixed,
        preferred_element_type=jnp.float32,
    )
    return jnp.stack([grad_query, grad_key, grad_value]).astype(jnp.bfloat16)


def slot_attend(packed, lengths_row):
    head_count = packed.shape[1]

    def whole_slot(operand):
        blocked = operand.reshape(3, head_count, 1, SLOT, HDIM)
        mixed_out, log_totals = block_forward(
            blocked[0], blocked[1], blocked[2], slot_allowed(lengths_row)
        )
        return (mixed_out.reshape(head_count, SLOT * HDIM), log_totals.reshape(head_count, SLOT))

    return whole_slot(packed)


def slot_attend_back(packed, grad_mixed, log_totals, lengths_row):
    head_count = packed.shape[1]

    def whole_slot(operands):
        blocked = operands[0].reshape(3, head_count, 1, SLOT, HDIM)
        result = block_backward(
            blocked[0],
            blocked[1],
            blocked[2],
            slot_allowed(lengths_row),
            operands[1].reshape(head_count, 1, SLOT, HDIM),
            operands[2].reshape(head_count, 1, SLOT),
        )
        return result.reshape(3, head_count, SLOT * HDIM)

    return whole_slot((packed, grad_mixed, log_totals))


def forward_slot(operands):
    return slot_attend(operands[0], operands[1])


def backward_slot(operands):
    return slot_attend_back(operands[0], operands[1], operands[2], operands[3])


def per_device(
    inputs,
    norm_gains,
    norm_shifts,
    w_qkv,
    qv_bias,
    w_out,
    out_biases,
    w_up,
    up_bias,
    w_down,
    lengths,
    d_out,
):
    groups = lax.axis_size("head")
    group_index = lax.axis_index("head")
    slot_count = inputs.shape[0]
    row_count = inputs.shape[1]
    local_heads = HEADS // groups
    gains = norm_gains.astype(jnp.float32)
    shifts = norm_shifts.astype(jnp.float32)
    biases = out_biases.astype(jnp.float32)
    up_shift = up_bias.astype(jnp.float32)
    query_bias = qv_bias.astype(jnp.float32)
    tokens = inputs.astype(jnp.float32)
    first_unit, first_inverse, first_normed = norm_parts(tokens, gains[0], shifts[0])
    normed_one = first_normed.astype(jnp.bfloat16)
    qkv_weight = w_qkv.reshape(D, 3, groups, local_heads, HDIM)
    full_bias = jnp.stack([query_bias[0], jnp.zeros_like(query_bias[0]), query_bias[1]])
    bias_grid = full_bias.reshape(3, groups, local_heads, HDIM).transpose(1, 0, 2, 3)[
        :, :, :, None, :
    ]
    projected = jnp.einsum(
        "srd,dcghe->sgchre", normed_one, qkv_weight, preferred_element_type=jnp.float32
    )
    packed = (
        (projected + bias_grid)
        .astype(jnp.bfloat16)
        .reshape(slot_count, groups, 3, local_heads, row_count * HDIM)
    )
    heads_side = lax.all_to_all(packed, "head", split_axis=1, concat_axis=4, tiled=True)[:, 0]
    mixed_heads, log_totals = lax.map(forward_slot, (heads_side, lengths))
    mixed_patch = lax.all_to_all(
        mixed_heads[:, None], "head", split_axis=3, concat_axis=1, tiled=True
    )
    mixed_patch = mixed_patch.reshape(slot_count, groups, local_heads, row_count, HDIM)
    out_weight = w_out.reshape(groups, local_heads, HDIM, D)
    attention = jnp.einsum(
        "sghre,ghef->srf", mixed_patch, out_weight, preferred_element_type=jnp.float32
    )
    hidden = (tokens + attention + biases[0]).reshape(-1, D)
    second_unit, second_inverse, second_normed = norm_parts(hidden, gains[1], shifts[1])
    normed_two = second_normed.astype(jnp.bfloat16)
    up_values = jnp.dot(normed_two, w_up, preferred_element_type=jnp.float32) + up_shift
    gelu_values, gelu_back = jax.vjp(exact_gelu, up_values)
    activated = gelu_values.astype(jnp.bfloat16)
    down_values = jnp.dot(activated, w_down, preferred_element_type=jnp.float32)
    block_out = (
        (hidden + down_values + biases[1]).astype(jnp.bfloat16).reshape(slot_count, row_count, D)
    )
    positions = group_index * row_count + jnp.arange(row_count, dtype=jnp.int32)
    totals = jnp.sum(lengths, axis=1)
    is_real = (positions[None, :] < totals[:, None]).astype(jnp.float32)
    grad_block = (d_out.astype(jnp.float32) * is_real[:, :, None]).reshape(-1, D)
    grad_low = grad_block.astype(jnp.bfloat16)
    down_grad = jnp.einsum("tf,td->fd", activated, grad_low, preferred_element_type=jnp.float32)
    grad_activated = jnp.einsum("td,fd->tf", grad_low, w_down, preferred_element_type=jnp.float32)
    grad_up = gelu_back(grad_activated)[0]
    grad_up_low = grad_up.astype(jnp.bfloat16)
    up_grad = jnp.einsum("td,tf->df", normed_two, grad_up_low, preferred_element_type=jnp.float32)
    upb_grad = jnp.sum(grad_up, axis=0)
    grad_normed_two = jnp.einsum("tf,df->td", grad_up_low, w_up, preferred_element_type=jnp.float32)
    grad_hidden = grad_block + norm_back(grad_normed_two, second_unit, second_inverse, gains[1])
    grad_hidden_low = grad_hidden.astype(jnp.bfloat16).reshape(slot_count, row_count, D)
    out_grad = jnp.einsum(
        "sghre,srf->ghef", mixed_patch, grad_hidden_low, preferred_element_type=jnp.float32
    ).reshape(D, D)
    grad_mixed = jnp.einsum(
        "srf,ghef->sghre", grad_hidden_low, out_weight, preferred_element_type=jnp.float32
    )
    grad_mixed = grad_mixed.astype(jnp.bfloat16).reshape(
        slot_count, groups, local_heads, row_count * HDIM
    )
    grad_heads = lax.all_to_all(grad_mixed, "head", split_axis=1, concat_axis=3, tiled=True)[:, 0]
    grad_packed = lax.map(backward_slot, (heads_side, grad_heads, log_totals, lengths))
    grad_patch = lax.all_to_all(
        grad_packed[:, None], "head", split_axis=4, concat_axis=1, tiled=True
    )
    grad_patch = grad_patch.reshape(slot_count, groups, 3, local_heads, row_count, HDIM)
    qkv_grad = jnp.einsum(
        "srd,sgchre->dcghe", normed_one, grad_patch, preferred_element_type=jnp.float32
    ).reshape(D, 3 * D)
    bias_sums = jnp.sum(grad_patch, axis=(0, 4), dtype=jnp.float32)
    bias_rows = bias_sums.transpose(1, 0, 2, 3).reshape(3, D)
    qv_grad = jnp.stack([bias_rows[0], bias_rows[2]])
    grad_normed_one = jnp.einsum(
        "sgchre,dcghe->srd", grad_patch, qkv_weight, preferred_element_type=jnp.float32
    )
    grad_inputs = grad_hidden.reshape(slot_count, row_count, D) + norm_back(
        grad_normed_one, first_unit, first_inverse, gains[0]
    )
    gains_grad = jnp.stack(
        [
            jnp.sum(grad_normed_one * first_unit, axis=(0, 1)),
            jnp.sum(grad_normed_two * second_unit, axis=0),
        ]
    )
    shifts_grad = jnp.stack(
        [jnp.sum(grad_normed_one, axis=(0, 1)), jnp.sum(grad_normed_two, axis=0)]
    )
    outb_grad = jnp.stack([jnp.sum(grad_hidden, axis=0), jnp.sum(grad_block, axis=0)])
    shared = (
        lax.psum_scatter(gains_grad, "dp", scatter_dimension=1, tiled=True),
        lax.psum_scatter(shifts_grad, "dp", scatter_dimension=1, tiled=True),
        lax.psum_scatter(qkv_grad, "dp", scatter_dimension=1, tiled=True),
        lax.psum_scatter(qv_grad, "dp", scatter_dimension=1, tiled=True),
        lax.psum_scatter(out_grad, "dp", scatter_dimension=1, tiled=True),
        lax.psum_scatter(outb_grad, "dp", scatter_dimension=1, tiled=True),
        lax.psum_scatter(up_grad, "dp", scatter_dimension=1, tiled=True),
        lax.psum_scatter(upb_grad, "dp", scatter_dimension=0, tiled=True),
        lax.psum_scatter(down_grad, "dp", scatter_dimension=1, tiled=True),
    )
    summed = (
        lax.psum(shared[0].astype(jnp.bfloat16), "head").astype(jnp.float32),
        lax.psum(shared[1].astype(jnp.bfloat16), "head").astype(jnp.float32),
        lax.psum(shared[2].astype(jnp.bfloat16), "head").astype(jnp.float32),
        lax.psum(shared[3].astype(jnp.bfloat16), "head").astype(jnp.float32),
        lax.psum(shared[4].astype(jnp.bfloat16), "head").astype(jnp.float32),
        lax.psum(shared[5].astype(jnp.bfloat16), "head").astype(jnp.float32),
        lax.psum(shared[6].astype(jnp.bfloat16), "head").astype(jnp.float32),
        lax.psum(shared[7].astype(jnp.bfloat16), "head").astype(jnp.float32),
        lax.psum(shared[8].astype(jnp.bfloat16), "head").astype(jnp.float32),
    )
    return (
        block_out,
        grad_inputs,
        summed[0],
        summed[1],
        summed[2],
        summed[3],
        summed[4],
        summed[5],
        summed[6],
        summed[7],
        summed[8],
    )


def solution(mesh):
    placed = (
        P("dp", "head", None),
        P(),
        P(),
        P(),
        P(),
        P(),
        P(),
        P(),
        P(),
        P(),
        P("dp", None),
        P("dp", "head", None),
    )
    return jax.shard_map(
        per_device,
        mesh=mesh,
        in_specs=placed,
        out_specs=(
            P("dp", "head", None),
            P("dp", "head", None),
            P(None, "dp"),
            P(None, "dp"),
            P(None, "dp"),
            P(None, "dp"),
            P(None, "dp"),
            P(None, "dp"),
            P(None, "dp"),
            P("dp"),
            P(None, "dp"),
        ),
        check_vma=False,
    )
```

profile of v0, /device:TPU:0, one launch (start us, length us, event | category | flops | bytes accessed | tf_op | source)
XLA Modules:
  0.0 1841.9 jit_solution(6899083665494931901)
XLA Ops:
  33.0 15.0 all-to-all-done
  68.8 50.4 %copy.160 = bf16[1,1,3,65536]{2,1,0,3:T(2,128)(2,1)} copy(bf16[1,1,3,65536]{3,2,1,0:T(4,128)(2,1)S(1)} %broadcast_in_dim.90) | data formatting | bytes 786432 | tf_op jit(solution)/shard_map/broadcast_in_dim | solution.py:169
  119.7 356.0 %reduce.28 = bf16[65536,3]{1,0:T(8,128)(2,1)} reduce(bf16[65536,1,1,3]{3,2,1,0:T(2,128)(2,1)} %bitcast.161, bf16[]{:T(256)} %broadcast.195), dimensions={1,2}, to_apply=%bitcast.124.reduce_sub_computation | reduce | bytes 786434
  475.7 33.0 %reshape.486 = bf16[4,2,24576]{2,1,0:T(2,128)(2,1)} reshape(bf16[65536,3]{1,0:T(8,128)(2,1)} %reduce.28) | data formatting | bytes 786432
  513.0 6.7 all-to-all-done.1
  519.7 51.9 %reshape.487 = bf16[65536,1,1,3]{3,2,1,0:T(2,128)(2,1)} reshape(bf16[4,2,24576]{2,1,0:T(2,128)(2,1)S(1)} %all-to-all-done.1) | data formatting | bytes 786432
  571.6 61.0 %copy.161 = bf16[1,1,3,65536]{3,2,1,0:T(4,128)(2,1)S(1)} copy(bf16[1,1,3,65536]{2,1,0,3:T(2,128)(2,1)} %bitcast.162) | data formatting | bytes 786432 | tf_op jit(solution)/shard_map/all_to_all | solution.py:168
  636.5 11.8 multiply_convert_fusion.1
  676.4 10.1 multiply_convert_fusion
  703.5 62.5 %copy.177 = bf16[1,1,3,3,65536]{3,2,1,0,4:T(4,128)(2,1)} copy(bf16[1,1,3,3,65536]{4,3,2,1,0:T(4,128)(2,1)S(1)} %pad_maximum_fusion) | data formatting | bytes 2359296 | tf_op jit(solution)/shard_map/while/body/eval_jaxpr/stack | solution.py:84
  766.0 88.2 %reshape.488 = bf16[4,2,73728]{2,1,0:T(2,128)(2,1)S(1)} reshape(bf16[65536,1,1,3,3]{4,3,2,1,0:T(4,128)(2,1)} %bitcast.126) | data formatting | bytes 2359296
  854.2 18.3 all_to_all.60
  872.5 89.1 %reshape.489 = bf16[65536,1,1,3,3]{4,3,2,1,0:T(4,128)(2,1)} reshape(bf16[4,2,73728]{2,1,0:T(2,128)(2,1)S(1)} %all_to_all.60) | data formatting | bytes 2359296
  961.6 90.3 %copy.178 = bf16[1,1,3,3,4,16384]{5,4,3,2,1,0:T(4,128)(2,1)} copy(bf16[1,1,3,3,4,16384]{3,2,5,4,1,0:T(4,128)(2,1)} %bitcast.30) | data formatting | bytes 2359296 | tf_op jit(solution)/shard_map/all_to_all | solution.py:211
  1068.8 6.7 fusion.57
  1101.1 89.4 %reduce-scatter.17.cloned.1.call-done = f32[768,288]{0,1:T(8,128)} async-done(((f32[768,2304]{0,1:T(8,128)}), f32[768,288]{0,1:T(8,128)}) %reduce-scatter.17.cloned.1.call-update) | async-done | bytes 884752 | tf_op jit(solution)/shard_map/reduce_scatter | solution.py:240
  1192.4 164.4 %reduce-scatter.21.cloned.1.call-done = f32[768,384]{1,0:T(8,128)} async-done(((f32[768,3072]{1,0:T(8,128)}), f32[768,384]{1,0:T(8,128)}) %reduce-scatter.21.cloned.1.call-update) | async-done | bytes 1179664 | tf_op jit(solution)/shard_map/reduce_scatter | solution.py:244
  1359.0 164.3 %reduce-scatter.23.cloned.1.call-done = f32[3072,96]{0,1:T(8,128)} async-done(((f32[3072,768]{0,1:T(8,128)}), f32[3072,96]{0,1:T(8,128)}) %reduce-scatter.23.cloned.1.call-update) | async-done | bytes 1179664 | tf_op jit(solution)/shard_map/reduce_scatter | solution.py:246
  1530.6 35.1 %all-reduce = bf16[3072]{0:T(1024)(128)(2,1)S(1)} all-reduce(f32[3072]{0:T(1024)S(1)} %copy-done.33), channel_id=9, replica_groups=mesh['dp'=8,'head'=4] {'dp'}, use_global_device_ids=true, to_apply=%region_36.37.clone | all-reduce | flops 3072 | bytes 18432
  1565.9 21.5 %reduce-scatter.31.cloned.1.call-done = f32[96,2]{1,0:T(8,128)} async-done(((f32[768,2]{1,0:T(8,128)}), f32[96,2]{1,0:T(8,128)}) %reduce-scatter.31.cloned.1.call-update) | async-done | bytes 784
  1589.5 61.9 %reduce-scatter.29.cloned.1.call-done = f32[96,2]{1,0:T(8,128)} async-done(((f32[768,2]{1,0:T(8,128)}), f32[96,2]{1,0:T(8,128)}) %reduce-scatter.29.cloned.1.call-update) | async-done | bytes 784
  1652.2 63.1 %reduce-scatter.27.cloned.1.call-done = f32[96,2]{1,0:T(8,128)} async-done(((f32[768,2]{1,0:T(8,128)}), f32[96,2]{1,0:T(8,128)}) %reduce-scatter.27.cloned.1.call-update) | async-done | bytes 784
  1716.2 63.2 %reduce-scatter.25.cloned.1.call-done = f32[96,2]{1,0:T(8,128)} async-done(((f32[768,2]{1,0:T(8,128)}), f32[96,2]{1,0:T(8,128)}) %reduce-scatter.25.cloned.1.call-update) | async-done | bytes 784
  1788.7 40.3 %all-reduce.5.cloned.1.call-done = (bf16[768,288]{0,1:T(8,128)(2,1)}, bf16[768,96]{0,1:T(8,128)(2,1)}, bf16[768,384]{1,0:T(8,128)(2,1)}, bf16[3072,96]{0,1:T(8,128)(2,1)}) async-done(((bf16[768,288]{0,1:T(8,128)(2,1)}, bf16[768,96]{0,1:T(8,128)(2,1)}, bf16[768,384]{1,0:T(8,128)(2,1)}, bf16[3072,96]{0,1:T(8,128)(2,1)}), (bf16[768,288]{0,1:T(8,128)(2,1)}, bf16[768,96]{0,1:T(8,128)(2,1)}, ...) | async-done | bytes 1769488 | tf_op jit(solution)/shard_map/psum | solution.py:251
  (254 shorter events, 172.3 us)
Async XLA Ops:
  7.2 628.4 %copy-start = (bf16[768,768]{1,0:T(8,128)(2,1)S(1)}, bf16[768,768]{1,0:T(8,128)(2,1)}, u32[]{:S(2)}) copy-start(bf16[768,768]{1,0:T(8,128)(2,1)} %param.17) | copy-start | bytes 3538948
  23.1 24.9 %all-to-all-start = ((bf16[1,4,3,3,16384]{4,3,2,0,1:T(4,128)(2,1)}), bf16[1,4,3,3,16384]{4,3,2,0,1:T(4,128)(2,1)S(1)}, u32[]{:S(2)}, u32[]{:S(2)}) async-start(bf16[1,4,3,3,16384]{4,3,2,0,1:T(4,128)(2,1)} %reshape.468), calls=%async_computation | async-start | bytes 3145728 | tf_op jit(solution)/shard_map/all_to_all | solution.py:166
  508.7 11.1 all-to-all-start.1
  513.0 140.4 %copy-start.24 = (f32[256]{0:T(256)}, f32[256]{0:T(256)S(1)}, u32[]{:S(2)}) copy-start(f32[256]{0:T(256)S(1)} %compare_convert_fusion) | copy-start | bytes 3076
  571.6 64.0 %copy-start.8 = (bf16[1,256,768]{2,1,0:T(8,128)(2,1)S(1)}, bf16[1,256,768]{2,1,0:T(8,128)(2,1)}, u32[]{:S(2)}) copy-start(bf16[1,256,768]{2,1,0:T(8,128)(2,1)} %param.12) | copy-start | bytes 1179652
  656.7 12.3 all-to-all-start.2
  660.2 439.2 %reduce-scatter.19.cloned.1.call-start = ((), (), s32[]{:S(2)}) async-start(), calls=%async_computation.13 | async-start | bytes 2654208 | tf_op jit(solution)/shard_map/reduce_scatter | solution.py:242
  663.6 526.8 %reduce-scatter.17.cloned.1.call-start = ((), (), s32[]{:S(2)}) async-start(), calls=%async_computation.12 | async-start | bytes 7962624 | tf_op jit(solution)/shard_map/reduce_scatter | solution.py:240
  670.0 23.7 %slice-start = ((s8[12582912]{0:T(1024)(128)(4,1)}), s8[4194304]{0:T(1024)(128)(4,1)S(1)}, s32[]{:S(2)}) async-start(s8[12582912]{0:T(1024)(128)(4,1)} %bitcast.159), calls=%async_computation.21 | async-start | bytes 8388608
  670.0 23.7 %slice-start.1 = ((s8[12582912]{0:T(1024)(128)(4,1)}), s8[4194304]{0:T(1024)(128)(4,1)S(1)}, s32[]{:S(2)}) async-start(s8[12582912]{0:T(1024)(128)(4,1)} %bitcast.159), calls=%async_computation.22 | async-start | bytes 8388608
  1060.3 296.5 %reduce-scatter.21.cloned.1.call-start = ((), (), s32[]{:S(2)}) async-start(), calls=%async_computation.14 | async-start | bytes 10616832 | tf_op jit(solution)/shard_map/reduce_scatter | solution.py:244
  1068.1 455.2 %reduce-scatter.23.cloned.1.call-start = ((), (), s32[]{:S(2)}) async-start(), calls=%async_computation.15 | async-start | bytes 10616832 | tf_op jit(solution)/shard_map/reduce_scatter | solution.py:246
  1075.5 511.8 %reduce-scatter.31.cloned.1.call-start = ((), (), s32[]{:S(2)}) async-start(), calls=%async_computation.19 | async-start | bytes 442368
  1086.0 565.3 %reduce-scatter.29.cloned.1.call-start = ((), (), s32[]{:S(2)}) async-start(), calls=%async_computation.18 | async-start | bytes 442368
  1095.3 620.1 %reduce-scatter.27.cloned.1.call-start = ((), (), s32[]{:S(2)}) async-start(), calls=%async_computation.17 | async-start | bytes 442368
  1097.0 682.3 %reduce-scatter.25.cloned.1.call-start = ((), (), s32[]{:S(2)}) async-start(), calls=%async_computation.16 | async-start | bytes 442368
  1098.1 730.9 %all-reduce.5.cloned.1.call-start = ((), (), s32[]{:S(2)}) async-start(), calls=%async_computation.20 | async-start | bytes 3538944 | tf_op jit(solution)/shard_map/psum | solution.py:251
  1101.1 424.4 %copy-start.42 = (f32[768]{0:T(1024)S(1)}, f32[768]{0:T(1024)}, u32[]{:S(2)}) copy-start(f32[768]{0:T(1024)} %get-tuple-element.52) | copy-start | bytes 9220
  1525.5 62.7 %copy-start.44 = (f32[256]{0:T(256)S(1)}, f32[256]{0:T(256)}, u32[]{:S(2)}) copy-start(f32[256]{0:T(256)} %get-tuple-element.47) | copy-start | bytes 3076
  1525.5 62.7 %copy-start.5 = (f32[256,768]{1,0:T(8,128)S(1)}, f32[256,768]{1,0:T(8,128)}, u32[]{:S(2)}) copy-start(f32[256,768]{1,0:T(8,128)} %copy-done.4) | copy-start | bytes 2359300
  1525.5 62.7 %copy-start.10 = (bf16[1,256,768]{2,1,0:T(8,128)(2,1)S(1)}, bf16[1,256,768]{2,1,0:T(8,128)(2,1)}, u32[]{:S(2)}) copy-start(bf16[1,256,768]{2,1,0:T(8,128)(2,1)} %param.12) | copy-start | bytes 1179652
  1525.5 62.7 %copy-start.16 = (f32[256,768,1,1,1]{1,0,4,3,2:T(8,128)S(1)}, f32[256,768,1,1,1]{1,0,4,3,2:T(8,128)}, u32[]{:S(2)}) copy-start(f32[256,768,1,1,1]{1,0,4,3,2:T(8,128)} %copy-done.15) | copy-start | bytes 2359300
  1525.5 62.7 %copy-start.40 = (f32[256]{0:T(256)S(1)}, f32[256]{0:T(256)}, u32[]{:S(2)}) copy-start(f32[256]{0:T(256)} %copy-done.38) | copy-start | bytes 3076
  1588.3 246.9 %copy-start.1 = (bf16[768,768]{1,0:T(8,128)(2,1)S(1)}, bf16[768,768]{1,0:T(8,128)(2,1)}, u32[]{:S(2)}) copy-start(bf16[768,768]{1,0:T(8,128)(2,1)} %param.17) | copy-start | bytes 3538948
  (42 other events, 279.8 us)
Sparse Core Ops, SparseCore 0:
  664.5 71.7 reduce-scatter.18
  1060.5 129.9 reduce-scatter.16
  1194.5 162.3 reduce-scatter.20
  1360.7 162.5 reduce-scatter.22
  1526.7 60.5 reduce-scatter.30
  1590.8 60.4 reduce-scatter.28
  1654.9 60.3 reduce-scatter.26
  1718.9 60.3 reduce-scatter.24
  1783.3 45.6 all-reduce.4
where the time goes:
time: 1850 us; the launch traced here: 1840 us
  waiting for transfers between devices  695 us (38%)
  local copies, waits for them, and re-layouts  587 us (32%)
  other arithmetic  401 us (22%)
  matrix products  71 us (4%)
  blocking collectives  59.1 us (3%)
    unnamed x4, other arithmetic  356 us
    unnamed x124, local copies, waits for them, and re-layouts  282 us
    unnamed x13, waiting for transfers between devices  210 us
    reduce_scatter x1, waiting for transfers between devices, per_device(): lax.psum_scatter(up_grad, 'dp', scatter_dimension=1, tiled=True)  164 us
    reduce_scatter x1, waiting for transfers between devices, per_device(): lax.psum_scatter(down_grad, 'dp', scatter_dimension=1, tiled=True)  164 us
    all_to_all x1, local copies, waits for them, and re-layouts, per_device(): lax.all_to_all(grad_packed[:, None], 'head', split_axis=4, concat_axis=1,...  90.3 us
    reduce_scatter x1, waiting for transfers between devices, per_device(): lax.psum_scatter(qkv_grad, 'dp', scatter_dimension=1, tiled=True)  89.4 us
    another operation x4, local copies, waits for them, and re-layouts, block_backward(): return jnp.stack([grad_query, grad_key, grad_value]).astype(jnp.bfloat16)  65.8 us
  transfers between devices with their start and end apart: 12, of which 11 were waited for; matrix products, arithmetic and copies ran while one was open for 24% of the time, Pallas kernels for 0%

commit v1 on v0

--- a/solution.py
+++ b/solution.py
@@ -165,8 +165,11 @@
     )
     heads_side = lax.all_to_all(packed, "head", split_axis=1, concat_axis=4, tiled=True)[:, 0]
     mixed_heads, log_totals = lax.map(forward_slot, (heads_side, lengths))
-    mixed_patch = lax.all_to_all(
-        mixed_heads[:, None], "head", split_axis=3, concat_axis=1, tiled=True
+    mixed_patch = jnp.concatenate(
+        lax.all_to_all(
+            jnp.stack(jnp.split(mixed_heads[:, None], lax.axis_size("head"), axis=3)), "head", 0, 0
+        ),
+        axis=1,
     )
     mixed_patch = mixed_patch.reshape(slot_count, groups, local_heads, row_count, HDIM)
     out_weight = w_out.reshape(groups, local_heads, HDIM, D)

time: 1850 us -> 1300 us (0.70)
  other arithmetic: 401 us -> 46.5 us
  local copies, waits for them, and re-layouts: 587 us -> 392 us
    unnamed x4 -> x3, other arithmetic: 356 us -> 0.01 us
    unnamed x124 -> x121, local copies, waits for them, and re-layouts: 282 us -> 197 us
    all_to_all x2 -> x1, local copies, waits for them, and re-layouts: 62.3 us -> 1.12 us  [per_device(): lax.all_to_all(jnp.stack(jnp.split(mixed_heads[:, None], lax.axis_size('h...]
    broadcast_in_dim x2 -> x1, local copies, waits for them, and re-layouts: 51 us -> 1.38 us  [per_device(): mixed_heads[:, None]]
  transfers between devices with their start and end apart: 12 -> 12, of which waited for: 11 -> 11; matrix products, arithmetic and copies ran while one was open for 24% -> 34% of each run, Pallas kernels for 0% -> 0%
where the time goes in v1:
time: 1300 us; the launch traced here: 1290 us
  waiting for transfers between devices  696 us (54%)
  local copies, waits for them, and re-layouts  392 us (30%)
  matrix products  70.5 us (5%)
  blocking collectives  59.1 us (5%)
  other arithmetic  46.5 us (4%)
  between operations  15.6 us (1%)
    unnamed x13, waiting for transfers between devices  210 us
    unnamed x121, local copies, waits for them, and re-layouts  197 us
    reduce_scatter x1, waiting for transfers between devices, per_device(): lax.psum_scatter(up_grad, 'dp', scatter_dimension=1, tiled=True)  164 us
    reduce_scatter x1, waiting for transfers between devices, per_device(): lax.psum_scatter(down_grad, 'dp', scatter_dimension=1, tiled=True)  164 us
    all_to_all x1, local copies, waits for them, and re-layouts, per_device(): lax.all_to_all(grad_packed[:, None], 'head', split_axis=4, concat_axis=1,...  90.3 us
    reduce_scatter x1, waiting for transfers between devices, per_device(): lax.psum_scatter(qkv_grad, 'dp', scatter_dimension=1, tiled=True)  89.4 us
    another operation x4, local copies, waits for them, and re-layouts, block_backward(): return jnp.stack([grad_query, grad_key, grad_value]).astype(jnp.bfloat16)  65.8 us
    psum x1, waiting for transfers between devices, per_device(): lax.psum(shared[2].astype(jnp.bfloat16), 'head').astype(jnp.float32)  40.2 us
  transfers between devices with their start and end apart: 12, of which 11 were waited for; matrix products, arithmetic and copies ran while one was open for 34% of the time, Pallas kernels for 0%

profile of v1, /device:TPU:0, one launch (start us, length us, event | category | flops | bytes accessed | tf_op | source)
XLA Modules:
  0.0 1292.9 jit_solution(18240997387236982717)
XLA Ops:
  32.7 15.0 %all-to-all-done = bf16[1,4,3,3,16384]{4,3,2,0,1:T(4,128)(2,1)S(1)} async-done(((bf16[1,4,3,3,16384]{4,3,2,0,1:T(4,128)(2,1)}), bf16[1,4,3,3,16384]{4,3,2,0,1:T(4,128)(2,1)S(1)}, u32[]{:S(2)}, u32[]{:S(2)}) %all-to-all-start) | async-done | bytes 1179680 | tf_op jit(solution)/shard_map/all_to_all | solution.py:166
  76.3 8.1 all-to-all-done.1
  88.2 11.5 multiply_convert_fusion.1
  121.3 6.2 multiply_reduce_fusion
  127.5 10.1 multiply_convert_fusion
  137.6 5.1 fusion.23
  154.6 62.5 %copy.141 = bf16[1,1,3,3,65536]{3,2,1,0,4:T(4,128)(2,1)} copy(bf16[1,1,3,3,65536]{4,3,2,1,0:T(4,128)(2,1)S(1)} %pad_maximum_fusion) | data formatting | bytes 2359296 | tf_op jit(solution)/shard_map/while/body/eval_jaxpr/stack | solution.py:84
  217.0 88.2 %reshape.484 = bf16[4,2,73728]{2,1,0:T(2,128)(2,1)S(1)} reshape(bf16[65536,1,1,3,3]{4,3,2,1,0:T(4,128)(2,1)} %bitcast.131) | data formatting | bytes 2359296
  305.2 18.3 %all_to_all.50 = bf16[4,2,73728]{2,1,0:T(2,128)(2,1)S(1)} all-to-all(bf16[4,2,73728]{2,1,0:T(2,128)(2,1)S(1)} %reshape.484), channel_id=1, replica_groups=mesh['dp'=8,'head'=4] {'head'}, dimensions={0} | all-to-all | bytes 2359296 | tf_op jit(solution)/shard_map/all_to_all | solution.py:214
  323.5 89.1 %reshape.485 = bf16[65536,1,1,3,3]{4,3,2,1,0:T(4,128)(2,1)} reshape(bf16[4,2,73728]{2,1,0:T(2,128)(2,1)S(1)} %all_to_all.50) | data formatting | bytes 2359296
  412.6 90.3 %copy.142 = bf16[1,1,3,3,4,16384]{5,4,3,2,1,0:T(4,128)(2,1)} copy(bf16[1,1,3,3,4,16384]{3,2,5,4,1,0:T(4,128)(2,1)} %bitcast.33) | data formatting | bytes 2359296 | tf_op jit(solution)/shard_map/all_to_all | solution.py:214
  512.4 6.6 fusion.43
  519.8 6.7 fusion.57
  526.5 5.8 copy.114
  552.1 89.4 %reduce-scatter.17.cloned.1.call-done = f32[768,288]{0,1:T(8,128)} async-done(((f32[768,2304]{0,1:T(8,128)}), f32[768,288]{0,1:T(8,128)}) %reduce-scatter.17.cloned.1.call-update) | async-done | bytes 884752 | tf_op jit(solution)/shard_map/reduce_scatter | solution.py:243
  643.5 164.4 %reduce-scatter.21.cloned.1.call-done = f32[768,384]{1,0:T(8,128)} async-done(((f32[768,3072]{1,0:T(8,128)}), f32[768,384]{1,0:T(8,128)}) %reduce-scatter.21.cloned.1.call-update) | async-done | bytes 1179664 | tf_op jit(solution)/shard_map/reduce_scatter | solution.py:247
  810.1 164.3 %reduce-scatter.23.cloned.1.call-done = f32[3072,96]{0,1:T(8,128)} async-done(((f32[3072,768]{0,1:T(8,128)}), f32[3072,96]{0,1:T(8,128)}) %reduce-scatter.23.cloned.1.call-update) | async-done | bytes 1179664 | tf_op jit(solution)/shard_map/reduce_scatter | solution.py:249
  981.7 35.1 %all-reduce = bf16[3072]{0:T(1024)(128)(2,1)S(1)} all-reduce(f32[3072]{0:T(1024)S(1)} %copy-done.33), channel_id=9, replica_groups=mesh['dp'=8,'head'=4] {'dp'}, use_global_device_ids=true, to_apply=%region_36.37.clone | all-reduce | flops 3072 | bytes 18432
  1017.0 21.4 %reduce-scatter.31.cloned.1.call-done = f32[96,2]{1,0:T(8,128)} async-done(((f32[768,2]{1,0:T(8,128)}), f32[96,2]{1,0:T(8,128)}) %reduce-scatter.31.cloned.1.call-update) | async-done | bytes 784
  1040.5 61.8 %reduce-scatter.29.cloned.1.call-done = f32[96,2]{1,0:T(8,128)} async-done(((f32[768,2]{1,0:T(8,128)}), f32[96,2]{1,0:T(8,128)}) %reduce-scatter.29.cloned.1.call-update) | async-done | bytes 784
  1103.2 63.2 %reduce-scatter.27.cloned.1.call-done = f32[96,2]{1,0:T(8,128)} async-done(((f32[768,2]{1,0:T(8,128)}), f32[96,2]{1,0:T(8,128)}) %reduce-scatter.27.cloned.1.call-update) | async-done | bytes 784
  1167.2 63.2 %reduce-scatter.25.cloned.1.call-done = f32[96,2]{1,0:T(8,128)} async-done(((f32[768,2]{1,0:T(8,128)}), f32[96,2]{1,0:T(8,128)}) %reduce-scatter.25.cloned.1.call-update) | async-done | bytes 784
  1231.4 5.7 all-reduce.1
  1239.8 40.2 %all-reduce.5.cloned.1.call-done = (bf16[768,288]{0,1:T(8,128)(2,1)}, bf16[768,96]{0,1:T(8,128)(2,1)}, bf16[768,384]{1,0:T(8,128)(2,1)}, bf16[3072,96]{0,1:T(8,128)(2,1)}) async-done(((bf16[768,288]{0,1:T(8,128)(2,1)}, bf16[768,96]{0,1:T(8,128)(2,1)}, bf16[768,384]{1,0:T(8,128)(2,1)}, bf16[3072,96]{0,1:T(8,128)(2,1)}), (bf16[768,288]{0,1:T(8,128)(2,1)}, bf16[768,96]{0,1:T(8,128)(2,1)}, ...) | async-done | bytes 1769488 | tf_op jit(solution)/shard_map/psum | solution.py:254
  (250 shorter events, 145.1 us)
Async XLA Ops:
  7.2 80.0 %copy-start = (bf16[768,768]{1,0:T(8,128)(2,1)S(1)}, bf16[768,768]{1,0:T(8,128)(2,1)}, u32[]{:S(2)}) copy-start(bf16[768,768]{1,0:T(8,128)(2,1)} %param.17) | copy-start | bytes 3538948
  23.1 24.6 %all-to-all-start = ((bf16[1,4,3,3,16384]{4,3,2,0,1:T(4,128)(2,1)}), bf16[1,4,3,3,16384]{4,3,2,0,1:T(4,128)(2,1)S(1)}, u32[]{:S(2)}, u32[]{:S(2)}) async-start(bf16[1,4,3,3,16384]{4,3,2,0,1:T(4,128)(2,1)} %reshape.466), calls=%async_computation | async-start | bytes 3145728 | tf_op jit(solution)/shard_map/all_to_all | solution.py:166
  67.9 19.3 %copy-start.8 = (bf16[1,256,768]{2,1,0:T(8,128)(2,1)S(1)}, bf16[1,256,768]{2,1,0:T(8,128)(2,1)}, u32[]{:S(2)}) copy-start(bf16[1,256,768]{2,1,0:T(8,128)(2,1)} %param.12) | copy-start | bytes 1179652
  71.9 12.5 all-to-all-start.1
  76.2 28.4 %copy-start.24 = (f32[256]{0:T(256)}, f32[256]{0:T(256)S(1)}, u32[]{:S(2)}) copy-start(f32[256]{0:T(256)S(1)} %compare_convert_fusion) | copy-start | bytes 3076
  108.0 12.3 all-to-all-start.2
  111.5 439.0 %reduce-scatter.19.cloned.1.call-start = ((), (), s32[]{:S(2)}) async-start(), calls=%async_computation.13 | async-start | bytes 2654208 | tf_op jit(solution)/shard_map/reduce_scatter | solution.py:245
  114.9 526.6 %reduce-scatter.17.cloned.1.call-start = ((), (), s32[]{:S(2)}) async-start(), calls=%async_computation.12 | async-start | bytes 7962624 | tf_op jit(solution)/shard_map/reduce_scatter | solution.py:243
  121.3 23.4 %slice-start = ((s8[12582912]{0:T(1024)(128)(4,1)}), s8[4194304]{0:T(1024)(128)(4,1)S(1)}, s32[]{:S(2)}) async-start(s8[12582912]{0:T(1024)(128)(4,1)} %bitcast.164), calls=%async_computation.21 | async-start | bytes 8388608
  121.3 23.4 %slice-start.1 = ((s8[12582912]{0:T(1024)(128)(4,1)}), s8[4194304]{0:T(1024)(128)(4,1)S(1)}, s32[]{:S(2)}) async-start(s8[12582912]{0:T(1024)(128)(4,1)} %bitcast.164), calls=%async_computation.22 | async-start | bytes 8388608
  511.3 296.6 %reduce-scatter.21.cloned.1.call-start = ((), (), s32[]{:S(2)}) async-start(), calls=%async_computation.14 | async-start | bytes 10616832 | tf_op jit(solution)/shard_map/reduce_scatter | solution.py:247
  519.1 455.3 %reduce-scatter.23.cloned.1.call-start = ((), (), s32[]{:S(2)}) async-start(), calls=%async_computation.15 | async-start | bytes 10616832 | tf_op jit(solution)/shard_map/reduce_scatter | solution.py:249
  526.5 511.9 %reduce-scatter.31.cloned.1.call-start = ((), (), s32[]{:S(2)}) async-start(), calls=%async_computation.19 | async-start | bytes 442368
  537.0 565.3 %reduce-scatter.29.cloned.1.call-start = ((), (), s32[]{:S(2)}) async-start(), calls=%async_computation.18 | async-start | bytes 442368
  546.3 620.1 %reduce-scatter.27.cloned.1.call-start = ((), (), s32[]{:S(2)}) async-start(), calls=%async_computation.17 | async-start | bytes 442368
  548.0 682.4 %reduce-scatter.25.cloned.1.call-start = ((), (), s32[]{:S(2)}) async-start(), calls=%async_computation.16 | async-start | bytes 442368
  549.1 731.0 %all-reduce.5.cloned.1.call-start = ((), (), s32[]{:S(2)}) async-start(), calls=%async_computation.20 | async-start | bytes 3538944 | tf_op jit(solution)/shard_map/psum | solution.py:254
  552.1 424.5 %copy-start.42 = (f32[768]{0:T(1024)S(1)}, f32[768]{0:T(1024)}, u32[]{:S(2)}) copy-start(f32[768]{0:T(1024)} %get-tuple-element.52) | copy-start | bytes 9220
  976.6 62.7 %copy-start.44 = (f32[256]{0:T(256)S(1)}, f32[256]{0:T(256)}, u32[]{:S(2)}) copy-start(f32[256]{0:T(256)} %get-tuple-element.47) | copy-start | bytes 3076
  976.6 62.7 %copy-start.5 = (f32[256,768]{1,0:T(8,128)S(1)}, f32[256,768]{1,0:T(8,128)}, u32[]{:S(2)}) copy-start(f32[256,768]{1,0:T(8,128)} %copy-done.4) | copy-start | bytes 2359300
  976.6 62.7 %copy-start.10 = (bf16[1,256,768]{2,1,0:T(8,128)(2,1)S(1)}, bf16[1,256,768]{2,1,0:T(8,128)(2,1)}, u32[]{:S(2)}) copy-start(bf16[1,256,768]{2,1,0:T(8,128)(2,1)} %param.12) | copy-start | bytes 1179652
  976.6 62.7 %copy-start.16 = (f32[256,768,1,1,1]{1,0,4,3,2:T(8,128)S(1)}, f32[256,768,1,1,1]{1,0,4,3,2:T(8,128)}, u32[]{:S(2)}) copy-start(f32[256,768,1,1,1]{1,0,4,3,2:T(8,128)} %copy-done.15) | copy-start | bytes 2359300
  976.6 62.7 %copy-start.40 = (f32[256]{0:T(256)S(1)}, f32[256]{0:T(256)}, u32[]{:S(2)}) copy-start(f32[256]{0:T(256)} %copy-done.38) | copy-start | bytes 3076
  1039.3 246.9 %copy-start.1 = (bf16[768,768]{1,0:T(8,128)(2,1)S(1)}, bf16[768,768]{1,0:T(8,128)(2,1)}, u32[]{:S(2)}) copy-start(bf16[768,768]{1,0:T(8,128)(2,1)} %param.17) | copy-start | bytes 3538948
  (42 other events, 276.2 us)
Sparse Core Ops, SparseCore 0:
  115.8 71.6 reduce-scatter.18
  511.5 130.0 reduce-scatter.16
  645.5 162.3 reduce-scatter.20
  811.8 162.5 reduce-scatter.22
  977.9 60.4 reduce-scatter.30
  1041.8 60.4 reduce-scatter.28
  1105.9 60.4 reduce-scatter.26
  1170.0 60.4 reduce-scatter.24
  1234.4 45.6 all-reduce.4
